TPU v7x, 32 devices: a whole 2x2x4 slice. The times are simulated.
32 devices in a mesh: fsdp: 8 (over z, y), rep: 4 (over x, core).
Axes of the slice: x: 2, y: 2, z: 4, core: 2. Of those that a mesh axis runs over, the one named last changes fastest.
Arguments:
- partial_grad: bfloat16 [4, 8, 1024, 1024], P('rep', None, 'fsdp'), may hold values from -3 to 3
- owner_table: int32 [8, 2], replicated, may hold values from -1 to 7, as said below
- left_stat: float32 [8, 2, 1024, 1024], P('fsdp', None, None, 'rep'), may hold values from -6 to 6
- right_stat: float32 [8, 2, 1024, 1024], P('fsdp', None, None, 'rep'), may hold values from -6 to 6
- left_root: bfloat16 [8, 2, 1024, 1024], P('fsdp', None, None, 'rep'), may hold values from -0.1875 to 0.1875
- right_root: bfloat16 [8, 2, 1024, 1024], P('fsdp', None, None, 'rep'), may hold values from -0.1875 to 0.1875
Outputs:
- left_new: float32 [8, 2, 1024, 1024], P('fsdp', None, None, 'rep')
- right_new: float32 [8, 2, 1024, 1024], P('fsdp', None, None, 'rep')
- update: bfloat16 [8, 1024, 1024], P(None, 'fsdp', 'rep')
Inputs may be any that keep to these rules, and one draw needn't show every extreme that they name: `owner_table`: each of the 8 blocks stands in exactly one slot and -1 marks an empty slot; some owner fills all 2 slots and some owner has none.
All inputs are finite; a program needn't handle non-finite values.
Results may differ from a plain program's by a relative error of at most 0.014.
Values may be sent and summed in bfloat16 or wider, within the bound.
No kernel may reach another device: no remote copies, remote signals or barrier semaphores. Data moves between devices by JAX's collectives and lax.ppermute only.
A program may use at most 64 MiB of HBM per device.

v0:
```python
import jax
import jax.numpy as jnp
from jax import lax
from jax.sharding import PartitionSpec as P

decay_rate = 0.99


def on_device(partial_grad, owner_table, left_stat, right_stat, left_root, right_root):
    local_grad = partial_grad[0]
    block_count = local_grad.shape[0]
    my_row = lax.dynamic_index_in_dim(owner_table, lax.axis_index("fsdp"), 0, keepdims=False)
    is_filled = my_row >= 0
    sender_index = jnp.maximum(owner_table.T, 0)
    sender_mask = owner_table.T >= 0
    shares = lax.psum_scatter(
        local_grad.astype(jnp.float32).astype(jnp.bfloat16), "rep", scatter_dimension=2, tiled=True
    )
    picked = jnp.take(shares, sender_index, axis=0)
    picked = jnp.where(sender_mask[:, :, None, None], picked, jnp.zeros((), picked.dtype))
    columns = lax.all_to_all(
        picked.reshape(picked.shape[0], -1, picked.shape[3]),
        "fsdp",
        split_axis=1,
        concat_axis=1,
        tiled=True,
    )
    gradient = lax.all_gather(columns, "rep", axis=2, tiled=True)
    share_width = left_stat.shape[3]
    first_col = lax.axis_index("rep") * share_width
    rows_share = lax.dynamic_slice_in_dim(gradient, first_col, share_width, 1)
    cols_share = lax.dynamic_slice_in_dim(gradient, first_col, share_width, 2)
    left_term = jnp.einsum("sik,sjk->sij", gradient, rows_share, preferred_element_type=jnp.float32)
    right_term = jnp.einsum(
        "ski,skj->sij", gradient, cols_share, preferred_element_type=jnp.float32
    )
    keeper = is_filled[:, None, None]
    left_next = jnp.where(
        keeper, decay_rate * left_stat[0] + (1.0 - decay_rate) * left_term, left_stat[0]
    )
    right_next = jnp.where(
        keeper, decay_rate * right_stat[0] + (1.0 - decay_rate) * right_term, right_stat[0]
    )
    applied = jnp.einsum(
        "sik,skj->sij",
        lax.all_gather(left_root[0], "rep", axis=2, tiled=True),
        gradient,
        preferred_element_type=jnp.float32,
    ).astype(jnp.bfloat16)
    result_cols = jnp.einsum(
        "sik,skj->sij", applied, right_root[0], preferred_element_type=jnp.float32
    ).astype(jnp.bfloat16)
    returned = lax.all_to_all(result_cols, "fsdp", split_axis=1, concat_axis=0, tiled=True)
    flat_table = owner_table.reshape(-1)
    slot_ids = jnp.arange(flat_table.shape[0], dtype=jnp.int32)
    block_ids = jnp.arange(block_count, dtype=jnp.int32)
    positions = jnp.sum(
        jnp.where(flat_table[None, :] == block_ids[:, None], slot_ids[None, :], 0), axis=1
    )
    update = jnp.take(returned, positions, axis=0)
    return (left_next[None], right_next[None], update)


def solution(mesh):
    return jax.shard_map(
        on_device,
        mesh=mesh,
        in_specs=(
            P("rep", None, "fsdp", None),
            P(),
            P("fsdp", None, None, "rep"),
            P("fsdp", None, None, "rep"),
            P("fsdp", None, None, "rep"),
            P("fsdp", None, None, "rep"),
        ),
        out_specs=(
            P("fsdp", None, None, "rep"),
            P("fsdp", None, None, "rep"),
            P(None, "fsdp", "rep"),
        ),
        check_vma=False,
    )
```

profile of v0, /device:TPU:0, one launch (start us, length us, event | category | flops | bytes accessed | tf_op | source)
XLA Modules:
  0.0 170.1 jit_solution(2735394884367178796)
XLA Ops:
  7.2 0.0 copy-start
  7.2 0.0 copy-start.1
  7.2 0.0 reduce-scatter.2.cloned.1.call-start
  7.2 0.7 reduce-scatter.2.cloned.1.call-update
  7.9 0.0 all-gather.6.cloned.1.call-start
  8.0 0.7 all-gather.6.cloned.1.call-update
  8.7 0.0 all-gather.4.cloned.1.call-start
  8.7 0.0 copy-done.1
  8.7 0.1 reshape.44
  8.9 0.1 broadcast_bitcast_fusion.1
  8.9 0.1 broadcast_bitcast_fusion
  9.0 35.4 %reduce-scatter.2.cloned.1.call-done = bf16[8,128,256]{2,1,0:T(8,128)(2,1)} async-done(((bf16[8,128,1024]{2,1,0:T(8,128)(2,1)}), bf16[8,128,256]{2,1,0:T(8,128)(2,1)}) %reduce-scatter.2.cloned.1.call-update) | async-done | bytes 524304 | tf_op jit(solution)/shard_map/reduce_scatter | solution.py:16
  44.4 1.7 gather_fusion
  46.1 0.9 fusion.18
  47.1 1.1 copy.31
  48.1 30.9 %all_to_all.23 = bf16[2,1024,256]{2,0,1:T(2,128)(2,1)S(1)} all-to-all(bf16[2,1024,256]{2,0,1:T(2,128)(2,1)S(1)} %copy.31), channel_id=1, replica_groups=mesh['fsdp'=8,'rep'=4] {'fsdp'}, dimensions={1} | all-to-all | bytes 2097152 | tf_op jit(solution)/shard_map/all_to_all | solution.py:21
  79.1 1.1 copy.32
  80.2 0.0 all-gather.4.cloned.1.call-update
  80.2 0.8 all-gather.6.cloned.1.call-done
  81.0 37.2 %all-gather.4.cloned.1.call-done = bf16[2,1024,1024]{2,1,0:T(8,128)(2,1)} async-done(((bf16[2,1024,256]{2,1,0:T(8,128)(2,1)}), bf16[2,1024,1024]{2,1,0:T(8,128)(2,1)}) %all-gather.4.cloned.1.call-update) | async-done | bytes 4194320 | tf_op jit(solution)/shard_map/all_gather | solution.py:28
  118.2 0.0 copy-done
  118.2 9.9 %fusion.12 = bf16[2,1024,256]{2,1,0:T(8,128)(2,1)S(1)} fusion(bf16[2,1024,1024]{2,1,0:T(8,128)(2,1)} %all-gather.4.cloned.1.call-done, bf16[1,2,1024,1024]{3,2,1,0:T(8,128)(2,1)} %all-gather.6.cloned.1.call-done, bf16[1,2,1024,256]{3,2,1,0:T(8,128)(2,1)S(1)} %copy-done), kind=kOutput, calls=%fused_computation.14 | convolution fusion | flops 5371330560 | bytes 10485760 | tf_op jit(solution)/shard_map/sik,skj->sij/dot_general | solution.py:50
  128.1 2.0 %copy.37 = bf16[2,1024,256]{2,0,1:T(2,128)(2,1)} copy(bf16[2,1024,256]{2,1,0:T(8,128)(2,1)S(1)} %fusion.12) | data formatting | bytes 2097152 | tf_op jit(solution)/shard_map/convert_element_type | solution.py:52
  130.1 5.5 %all-to-all-start.1 = ((bf16[2,1024,256]{2,0,1:T(2,128)(2,1)}), bf16[2,1024,256]{2,0,1:T(2,128)(2,1)S(1)}, u32[]{:S(2)}, u32[]{:S(2)}) async-start(bf16[2,1024,256]{2,0,1:T(2,128)(2,1)} %copy.37), calls=%async_computation.2 | async-start | bytes 2097152 | tf_op jit(solution)/shard_map/all_to_all | solution.py:53
  135.6 0.1 copy.34
  135.7 0.1 eq.15
  135.8 0.2 compare_reduce_fusion
  136.0 0.1 select_reduce_fusion
  136.1 0.0 copy-start.2
  136.2 0.0 copy-start.3
  136.2 6.4 %fusion.5 = f32[1,2,1024,256]{3,2,1,0:T(8,128)} fusion(f32[1,2,1024,256]{3,2,1,0:T(8,128)} %param.9, bf16[2,1024,1024]{2,1,0:T(8,128)(2,1)} %all-gather.4.cloned.1.call-done, s32[]{:T(128)S(6)} %select_n.55, pred[2]{0:T(512)(128)(4,1)S(1)} %compare_reduce_fusion), kind=kOutput, calls=%fused_computation.9 | convolution fusion | flops 1075838976 | bytes 9437190 | tf_op jit(solution)/shard_map/ski,skj->sij/dot_general | solution.py:34
  142.6 0.0 copy-done.2
  142.6 0.0 copy-done.3
  142.6 2.7 %fusion.7 = f32[1,2,1024,256]{3,2,1,0:T(8,128)} fusion(f32[1,2,1024,256]{3,2,1,0:T(8,128)S(1)} %copy-done.3, bf16[2,1024,1024]{2,1,0:T(8,128)(2,1)S(1)} %copy-done.2, s32[]{:T(128)S(6)} %select_n.55, pred[2]{0:T(512)(128)(4,1)S(1)} %compare_reduce_fusion), kind=kOutput, calls=%fused_computation.13 | convolution fusion | flops 1075838976 | bytes 9437700 | tf_op jit(solution)/shard_map/sik,sjk->sij/dot_general | solution.py:33
  145.4 16.5 %all-to-all-done.1 = bf16[2,1024,256]{2,0,1:T(2,128)(2,1)S(1)} async-done(((bf16[2,1024,256]{2,0,1:T(2,128)(2,1)}), bf16[2,1024,256]{2,0,1:T(2,128)(2,1)S(1)}, u32[]{:S(2)}, u32[]{:S(2)}) %all-to-all-start.1) | async-done | bytes 1048608 | tf_op jit(solution)/shard_map/all_to_all | solution.py:53
  161.8 0.1 copy.38
  162.0 0.1 copy.39
  162.1 0.6 gather_fusion.1
  162.7 0.9 broadcast_select_fusion
  (8 shorter events, 0.1 us)
Async XLA Ops:
  7.2 111.1 %copy-start = (bf16[1,2,1024,256]{3,2,1,0:T(8,128)(2,1)S(1)}, bf16[1,2,1024,256]{3,2,1,0:T(8,128)(2,1)}, u32[]{:S(2)}) copy-start(bf16[1,2,1024,256]{3,2,1,0:T(8,128)(2,1)} %param.11) | copy-start | bytes 3145732
  7.2 1.5 copy-start.1
  7.2 37.3 %reduce-scatter.2.cloned.1.call-start = ((), (), s32[]{:S(2)}) async-start(), calls=%async_computation.3 | async-start | bytes 2621440 | tf_op jit(solution)/shard_map/reduce_scatter | solution.py:16
  7.9 73.1 %all-gather.6.cloned.1.call-start = ((), (), s32[]{:S(2)}) async-start(), calls=%async_computation.5 | async-start | bytes 5242880 | tf_op jit(solution)/shard_map/all_gather | solution.py:46
  8.7 109.5 %all-gather.4.cloned.1.call-start = ((), (), s32[]{:S(2)}) async-start(), calls=%async_computation.4 | async-start | bytes 5242880 | tf_op jit(solution)/shard_map/all_gather | solution.py:28
  130.1 31.7 %all-to-all-start.1 = ((bf16[2,1024,256]{2,0,1:T(2,128)(2,1)}), bf16[2,1024,256]{2,0,1:T(2,128)(2,1)S(1)}, u32[]{:S(2)}, u32[]{:S(2)}) async-start(bf16[2,1024,256]{2,0,1:T(2,128)(2,1)} %copy.37), calls=%async_computation.2 | async-start | bytes 2097152 | tf_op jit(solution)/shard_map/all_to_all | solution.py:53
  136.1 6.5 %copy-start.2 = (bf16[2,1024,1024]{2,1,0:T(8,128)(2,1)S(1)}, bf16[2,1024,1024]{2,1,0:T(8,128)(2,1)}, u32[]{:S(2)}) copy-start(bf16[2,1024,1024]{2,1,0:T(8,128)(2,1)} %all-gather.4.cloned.1.call-done) | copy-start | bytes 12582916
  136.2 6.5 %copy-start.3 = (f32[1,2,1024,256]{3,2,1,0:T(8,128)S(1)}, f32[1,2,1024,256]{3,2,1,0:T(8,128)}, u32[]{:S(2)}) copy-start(f32[1,2,1024,256]{3,2,1,0:T(8,128)} %param.8) | copy-start | bytes 6291460
Sparse Core Ops, SparseCore 0:
  10.5 33.8 reduce-scatter.1
  46.0 34.9 all-gather.5
  83.2 34.9 all-gather.3
where the time goes:
time: 170 us
  waiting for transfers between devices  91.3 us (54%)
  blocking collectives  30.9 us (18%)
  matrix products  19 us (11%)
  between operations  13.9 us (8%)
  local copies, waits for them, and re-layouts  7.14 us (4%)
  starting transfers between devices  5.63 us (3%)
  other arithmetic  2.2 us (1%)
    all_gather x1, waiting for transfers between devices, on_device(): gradient = lax.all_gather(columns, 'rep', axis=2, tiled=True)  37.2 us
    reduce_scatter x1, waiting for transfers between devices, on_device(): lax.psum_scatter(local_grad.astype(jnp.float32).astype(jnp.bfloat16), 're...  35.4 us
    all_to_all x1, blocking collectives, on_device(): lax.all_to_all(picked.reshape(picked.shape[0], -1, picked.shape[3]), 'fsd...  30.9 us
    all_to_all x1, waiting for transfers between devices, on_device(): lax.all_to_all(result_cols, 'fsdp', split_axis=1, concat_axis=0, tiled=True)  16.5 us
    dot_general x1, matrix products, on_device(): jnp.einsum('sik,skj->sij', applied, right_root[0], preferred_element_type...  9.85 us
    dot_general x1, matrix products, on_device(): jnp.einsum('ski,skj->sij', gradient, cols_share, preferred_element_type=j...  6.45 us
    all_to_all x1, starting transfers between devices, on_device(): lax.all_to_all(result_cols, 'fsdp', split_axis=1, concat_axis=0, tiled=True)  5.52 us
  transfers between devices with their start and end apart: 4, of which 4 were waited for; matrix products, arithmetic and copies ran while one was open for 9% of the time, Pallas kernels for 0%

commit v1 on v0

--- a/solution.py
+++ b/solution.py
@@ -18,12 +18,20 @@
     )
     picked = jnp.take(shares, sender_index, axis=0)
     picked = jnp.where(sender_mask[:, :, None, None], picked, jnp.zeros((), picked.dtype))
-    columns = lax.all_to_all(
-        picked.reshape(picked.shape[0], -1, picked.shape[3]),
-        "fsdp",
-        split_axis=1,
-        concat_axis=1,
-        tiled=True,
+    columns = jnp.concatenate(
+        lax.all_to_all(
+            jnp.stack(
+                jnp.split(
+                    picked.reshape(picked.shape[0], -1, picked.shape[3]),
+                    lax.axis_size("fsdp"),
+                    axis=1,
+                )
+            ),
+            "fsdp",
+            0,
+            0,
+        ),
+        axis=1,
     )
     gradient = lax.all_gather(columns, "rep", axis=2, tiled=True)
     share_width = left_stat.shape[3]

time: 170 us -> 170 us (level)
  transfers between devices with their start and end apart: 4 -> 4, of which waited for: 4 -> 4; matrix products, arithmetic and copies ran while one was open for 9% -> 8% of each run, Pallas kernels for 0% -> 0%
where the time goes in v1:
time: 170 us
  waiting for transfers between devices  92.3 us (54%)
  blocking collectives  30.9 us (18%)
  matrix products  19 us (11%)
  between operations  13.9 us (8%)
  local copies, waits for them, and re-layouts  6.08 us (4%)
  starting transfers between devices  5.63 us (3%)
  other arithmetic  2.2 us (1%)
    all_gather x1, waiting for transfers between devices, on_device(): gradient = lax.all_gather(columns, 'rep', axis=2, tiled=True)  37.2 us
    reduce_scatter x1, waiting for transfers between devices, on_device(): lax.psum_scatter(local_grad.astype(jnp.float32).astype(jnp.bfloat16), 're...  35.4 us
    all_to_all x1, blocking collectives, on_device(): lax.all_to_all(jnp.stack(jnp.split(picked.reshape(picked.shape[0], -1, pi...  30.9 us
    all_to_all x1, waiting for transfers between devices, on_device(): lax.all_to_all(result_cols, 'fsdp', split_axis=1, concat_axis=0, tiled=True)  16.5 us
    dot_general x1, matrix products, on_device(): jnp.einsum('sik,skj->sij', applied, right_root[0], preferred_element_type...  9.85 us
    dot_general x1, matrix products, on_device(): jnp.einsum('ski,skj->sij', gradient, cols_share, preferred_element_type=j...  6.45 us
    all_to_all x1, starting transfers between devices, on_device(): lax.all_to_all(result_cols, 'fsdp', split_axis=1, concat_axis=0, tiled=True)  5.52 us
  transfers between devices with their start and end apart: 4, of which 4 were waited for; matrix products, arithmetic and copies ran while one was open for 8% of the time, Pallas kernels for 0%

profile of v1, /device:TPU:0, one launch (start us, length us, event | category | flops | bytes accessed | tf_op | source)
XLA Modules:
  0.0 170.1 jit_solution(8760038868949579486)
XLA Ops:
  7.2 0.0 copy-start
  7.2 0.0 copy-start.1
  7.2 0.0 reduce-scatter.2.cloned.1.call-start
  7.2 0.7 reduce-scatter.2.cloned.1.call-update
  7.9 0.0 all-gather.6.cloned.1.call-start
  8.0 0.7 all-gather.6.cloned.1.call-update
  8.7 0.0 all-gather.4.cloned.1.call-start
  8.7 0.0 copy-done.1
  8.7 0.1 reshape.52
  8.9 0.1 broadcast_bitcast_fusion.1
  8.9 0.1 broadcast_bitcast_fusion
  9.0 35.4 %reduce-scatter.2.cloned.1.call-done = bf16[8,128,256]{2,1,0:T(8,128)(2,1)} async-done(((bf16[8,128,1024]{2,1,0:T(8,128)(2,1)}), bf16[8,128,256]{2,1,0:T(8,128)(2,1)}) %reduce-scatter.2.cloned.1.call-update) | async-done | bytes 524304 | tf_op jit(solution)/shard_map/reduce_scatter | solution.py:16
  44.4 1.7 gather_fusion
  46.1 0.9 fusion.18
  47.2 30.9 %all_to_all.23 = bf16[8,2,128,256]{3,2,1,0:T(8,128)(2,1)S(1)} all-to-all(bf16[8,2,128,256]{3,2,1,0:T(8,128)(2,1)S(1)} %fusion.21), channel_id=1, replica_groups=mesh['fsdp'=8,'rep'=4] {'fsdp'}, dimensions={0} | all-to-all | bytes 2097152 | tf_op jit(solution)/shard_map/all_to_all | solution.py:22
  78.1 1.0 copy.42
  79.2 0.0 all-gather.4.cloned.1.call-update
  79.2 1.9 %all-gather.6.cloned.1.call-done = bf16[1,2,1024,1024]{3,2,1,0:T(8,128)(2,1)} async-done(((bf16[1,2,1024,256]{3,2,1,0:T(8,128)(2,1)}), bf16[1,2,1024,1024]{3,2,1,0:T(8,128)(2,1)}) %all-gather.6.cloned.1.call-update) | async-done | bytes 4194320 | tf_op jit(solution)/shard_map/all_gather | solution.py:54
  81.0 37.2 %all-gather.4.cloned.1.call-done = bf16[2,1024,1024]{2,1,0:T(8,128)(2,1)} async-done(((bf16[2,1024,256]{2,1,0:T(8,128)(2,1)}), bf16[2,1024,1024]{2,1,0:T(8,128)(2,1)}) %all-gather.4.cloned.1.call-update) | async-done | bytes 4194320 | tf_op jit(solution)/shard_map/all_gather | solution.py:36
  118.2 0.0 copy-done
  118.2 9.9 %fusion.12 = bf16[2,1024,256]{2,1,0:T(8,128)(2,1)S(1)} fusion(bf16[2,1024,1024]{2,1,0:T(8,128)(2,1)} %all-gather.4.cloned.1.call-done, bf16[1,2,1024,1024]{3,2,1,0:T(8,128)(2,1)} %all-gather.6.cloned.1.call-done, bf16[1,2,1024,256]{3,2,1,0:T(8,128)(2,1)S(1)} %copy-done), kind=kOutput, calls=%fused_computation.14 | convolution fusion | flops 5371330560 | bytes 10485760 | tf_op jit(solution)/shard_map/sik,skj->sij/dot_general | solution.py:58
  128.1 2.0 %copy.47 = bf16[2,1024,256]{2,0,1:T(2,128)(2,1)} copy(bf16[2,1024,256]{2,1,0:T(8,128)(2,1)S(1)} %fusion.12) | data formatting | bytes 2097152 | tf_op jit(solution)/shard_map/convert_element_type | solution.py:60
  130.1 5.5 %all-to-all-start.1 = ((bf16[2,1024,256]{2,0,1:T(2,128)(2,1)}), bf16[2,1024,256]{2,0,1:T(2,128)(2,1)S(1)}, u32[]{:S(2)}, u32[]{:S(2)}) async-start(bf16[2,1024,256]{2,0,1:T(2,128)(2,1)} %copy.47), calls=%async_computation.2 | async-start | bytes 2097152 | tf_op jit(solution)/shard_map/all_to_all | solution.py:61
  135.6 0.1 copy.44
  135.7 0.1 eq.15
  135.8 0.2 compare_reduce_fusion
  136.0 0.1 select_reduce_fusion
  136.1 0.0 copy-start.2
  136.1 0.0 copy-start.3
  136.2 6.4 %fusion.5 = f32[1,2,1024,256]{3,2,1,0:T(8,128)} fusion(f32[1,2,1024,256]{3,2,1,0:T(8,128)} %param.9, bf16[2,1024,1024]{2,1,0:T(8,128)(2,1)} %all-gather.4.cloned.1.call-done, s32[]{:T(128)S(6)} %select_n.55, pred[2]{0:T(512)(128)(4,1)S(1)} %compare_reduce_fusion), kind=kOutput, calls=%fused_computation.9 | convolution fusion | flops 1075838976 | bytes 9437190 | tf_op jit(solution)/shard_map/ski,skj->sij/dot_general | solution.py:42
  142.6 0.0 copy-done.2
  142.6 0.0 copy-done.3
  142.6 2.7 %fusion.7 = f32[1,2,1024,256]{3,2,1,0:T(8,128)} fusion(f32[1,2,1024,256]{3,2,1,0:T(8,128)S(1)} %copy-done.3, bf16[2,1024,1024]{2,1,0:T(8,128)(2,1)S(1)} %copy-done.2, s32[]{:T(128)S(6)} %select_n.55, pred[2]{0:T(512)(128)(4,1)S(1)} %compare_reduce_fusion), kind=kOutput, calls=%fused_computation.13 | convolution fusion | flops 1075838976 | bytes 9437700 | tf_op jit(solution)/shard_map/sik,sjk->sij/dot_general | solution.py:41
  145.4 16.5 %all-to-all-done.1 = bf16[2,1024,256]{2,0,1:T(2,128)(2,1)S(1)} async-done(((bf16[2,1024,256]{2,0,1:T(2,128)(2,1)}), bf16[2,1024,256]{2,0,1:T(2,128)(2,1)S(1)}, u32[]{:S(2)}, u32[]{:S(2)}) %all-to-all-start.1) | async-done | bytes 1048608 | tf_op jit(solution)/shard_map/all_to_all | solution.py:61
  161.8 0.1 copy.48
  162.0 0.1 copy.49
  162.1 0.6 gather_fusion.1
  162.7 0.9 broadcast_select_fusion
  (16 shorter events, 0.1 us)
Async XLA Ops:
  7.2 111.0 %copy-start = (bf16[1,2,1024,256]{3,2,1,0:T(8,128)(2,1)S(1)}, bf16[1,2,1024,256]{3,2,1,0:T(8,128)(2,1)}, u32[]{:S(2)}) copy-start(bf16[1,2,1024,256]{3,2,1,0:T(8,128)(2,1)} %param.11) | copy-start | bytes 3145732
  7.2 1.5 copy-start.1
  7.2 37.3 %reduce-scatter.2.cloned.1.call-start = ((), (), s32[]{:S(2)}) async-start(), calls=%async_computation.3 | async-start | bytes 2621440 | tf_op jit(solution)/shard_map/reduce_scatter | solution.py:16
  7.9 73.1 %all-gather.6.cloned.1.call-start = ((), (), s32[]{:S(2)}) async-start(), calls=%async_computation.5 | async-start | bytes 5242880 | tf_op jit(solution)/shard_map/all_gather | solution.py:54
  8.7 109.5 %all-gather.4.cloned.1.call-start = ((), (), s32[]{:S(2)}) async-start(), calls=%async_computation.4 | async-start | bytes 5242880 | tf_op jit(solution)/shard_map/all_gather | solution.py:36
  130.1 31.7 %all-to-all-start.1 = ((bf16[2,1024,256]{2,0,1:T(2,128)(2,1)}), bf16[2,1024,256]{2,0,1:T(2,128)(2,1)S(1)}, u32[]{:S(2)}, u32[]{:S(2)}) async-start(bf16[2,1024,256]{2,0,1:T(2,128)(2,1)} %copy.47), calls=%async_computation.2 | async-start | bytes 2097152 | tf_op jit(solution)/shard_map/all_to_all | solution.py:61
  136.1 6.5 %copy-start.2 = (bf16[2,1024,1024]{2,1,0:T(8,128)(2,1)S(1)}, bf16[2,1024,1024]{2,1,0:T(8,128)(2,1)}, u32[]{:S(2)}) copy-start(bf16[2,1024,1024]{2,1,0:T(8,128)(2,1)} %all-gather.4.cloned.1.call-done) | copy-start | bytes 12582916
  136.1 6.5 %copy-start.3 = (f32[1,2,1024,256]{3,2,1,0:T(8,128)S(1)}, f32[1,2,1024,256]{3,2,1,0:T(8,128)}, u32[]{:S(2)}) copy-start(f32[1,2,1024,256]{3,2,1,0:T(8,128)} %param.8) | copy-start | bytes 6291460
Sparse Core Ops, SparseCore 0:
  10.5 33.8 reduce-scatter.1
  46.0 34.9 all-gather.5
  83.2 34.9 all-gather.3
